TPU v7x, 256 devices: a whole 4x4x8 slice. The times are simulated.
256 devices in a mesh: leaf: 64 (over z, y, core), hand: 4 (over x).
Axes of the slice: x: 4, y: 4, z: 8, core: 2. Of those that a mesh axis runs over, the one named last changes fastest.
Arguments:
- opp_range: float32 [1024], P('hand'), may hold values from 0.1 to 1
- br_range: float32 [1024], P('hand'), may hold values from 0.001 to 1
- up_weight: bfloat16 [4, 2048, 1024], P(None, 'leaf', 'hand'), may hold values from 0.29882812 to 1
- up_parent: int32 [3, 2048], replicated, may hold values from 0 to 2047
- board_cards: int32 [6144, 5], P('leaf'), may hold values from 0 to 51, as said below
- hand_rank: int32 [6144, 1024], P('leaf'), may hold values from 0 to 7461
- root_parent: int32 [6144], P('leaf'), may hold values from 0 to 2047
- br_actions: int32 [6144], P('leaf'), may hold values from 1 to 8
- opp_actions: int32 [6144, 8], P('leaf'), may hold values from 1 to 8
- leaf_kind: int32 [6144, 8, 8], P('leaf'), may hold values from 0 to 1
- leaf_stake: int32 [6144, 8, 8], P('leaf'), may hold values from 1 to 400
- opp_weight: bfloat16 [6144, 8, 8, 1024], P('leaf', None, None, 'hand'), may hold values from 0.049804688 to 1
Outputs:
- level_values: float32 [4, 2048, 1024], P(None, 'leaf', 'hand')
- root_value: float32 [1024], P('hand')
- best_value: float32 [], replicated
Inputs may be any that keep to these rules, and one draw needn't show every extreme that they name: `board_cards`: five different cards for each subtree.
All inputs are finite; a program needn't handle non-finite values.
Results may differ from a plain program's by a relative error of at most 0.0003.
Values may be sent and summed in bfloat16 or wider, within the bound.
A program may use at most 128 MiB of HBM per device.

v0:
```python
import jax
import jax.numpy as jnp
import numpy as np
from jax import lax
from jax.sharding import Mesh
from jax.sharding import PartitionSpec as P

LEAF = ("leaf_0", "leaf_1", "leaf_2")


PAYOFF_UNIT = 1.0 / 4096.0


def laid_out(parts, dim):
    parts = jnp.moveaxis(parts, 0, dim)
    lengths = parts.shape
    return parts.reshape(*lengths[:dim], lengths[dim] * lengths[dim + 1], *lengths[dim + 2 :])


def all_blocks(x, axes, turns):
    parts = x[None]
    for k in turns:
        parts = lax.all_gather(parts, axes[k], axis=0, tiled=True)
    carried = [lax.axis_size(axes[k]) for k in reversed(turns)]
    parts = parts.reshape(*carried, *x.shape)
    turned = sorted(range(len(turns)), key=lambda place: turns[len(turns) - 1 - place])
    return parts.transpose(*turned, *range(len(turns), parts.ndim)).reshape(-1, *x.shape)


def whole_of(x, axes, turns, dim):
    return laid_out(all_blocks(x, axes, turns), dim)


def split_up(x, dim, devices):
    before, after = (x.shape[:dim], x.shape[dim + 1 :])
    return jnp.moveaxis(x.reshape(*before, devices, -1, *after), dim, 0)


def summed_on_arrival(x, axis, dim):
    parts = split_up(x, dim, lax.axis_size(axis))
    arrived = lax.all_to_all(parts, axis, split_axis=0, concat_axis=0, tiled=True)
    return arrived.sum(axis=0)


def copy_for_each(x, axis):
    devices = lax.axis_size(axis)
    return lax.all_to_all(jnp.broadcast_to(x[None], (devices, *x.shape)), axis, 0, 0, tiled=True)


def gather_directly(x, axis, dim):
    return laid_out(copy_for_each(x, axis), dim)


def of_everyone(x, axis):
    everything = copy_for_each(x, axis)
    return jnp.sum(everything, axis=0)


def hand_cards(number):
    low_list = []
    high_list = []
    for low_card in range(52):
        for high_card in range(low_card + 1, 52):
            low_list.append(low_card)
            high_list.append(high_card)
    chosen = np.arange(number) * 1326 // number
    return (np.array(low_list, np.int32)[chosen], np.array(high_list, np.int32)[chosen])


def no_shared(low_rows, high_rows, low_cols, high_cols):
    apart_mask = (low_rows[:, None] != low_cols[None, :]) & (
        low_rows[:, None] != high_cols[None, :]
    )
    apart_mask = (
        apart_mask
        & (high_rows[:, None] != low_cols[None, :])
        & (high_rows[:, None] != high_cols[None, :])
    )
    return apart_mask.astype(jnp.float32)


def board_compat(board_cards, low_cols, high_cols):
    hits = (board_cards[:, :, None] == low_cols[None, None, :]) | (
        board_cards[:, :, None] == high_cols[None, None, :]
    )
    return 1.0 - jnp.any(hits, axis=1).astype(jnp.float32)


def local(
    opp_range,
    br_range,
    up_weight,
    up_parent,
    board_cards,
    hand_rank,
    root_parent,
    br_actions,
    opp_actions,
    leaf_kind,
    leaf_stake,
    opp_weight,
):
    levels_count = up_weight.shape[0]
    nodes_dev = up_weight.shape[1]
    hands_dev = opp_range.shape[0]
    boards_dev = board_cards.shape[0]
    actions_max = opp_actions.shape[1]
    hands_all = hand_rank.shape[1]
    node_total = nodes_dev * lax.axis_size(LEAF)
    node_start = lax.axis_index(LEAF) * nodes_dev
    hand_start = lax.axis_index("hand") * hands_dev
    low_np, high_np = hand_cards(hands_all)
    low_all = jnp.asarray(low_np)
    high_all = jnp.asarray(high_np)
    low_mine = lax.dynamic_slice_in_dim(low_all, hand_start, hands_dev)
    high_mine = lax.dynamic_slice_in_dim(high_all, hand_start, hands_dev)
    compat = board_compat(board_cards, low_mine, high_mine)
    weights = whole_of(up_weight, LEAF, (1, 0, 2), 1)
    gathered = opp_range[None, :] * weights[0].astype(jnp.float32)
    for level_id in range(1, levels_count):
        gathered = jnp.take(gathered, up_parent[level_id - 1], axis=0) * weights[level_id].astype(
            jnp.float32
        )
    root_reach = jnp.take(gathered, root_parent, axis=0) * compat
    legal_mask = (jnp.arange(actions_max)[None, None, :] < opp_actions[:, :, None]).astype(
        jnp.float32
    )
    weighted = opp_weight.astype(jnp.float32) * legal_mask[..., None]
    probability = weighted / jnp.sum(weighted, axis=2, keepdims=True)
    leaf_reach = (root_reach[:, None, None, :] * probability).astype(jnp.bfloat16)
    leaf_reach = leaf_reach.reshape(boards_dev, actions_max * actions_max, hands_dev)
    kind_flat = leaf_kind.reshape(boards_dev, -1)
    stake_flat = leaf_stake.reshape(boards_dev, -1).astype(jnp.float32) * PAYOFF_UNIT
    rank_mine = lax.dynamic_slice_in_dim(hand_rank, hand_start, hands_dev, 1)
    zero_block = jnp.zeros(leaf_reach.shape, jnp.float32)
    block_rows = lax.all_gather(leaf_reach, "hand", axis=2, tiled=True)
    count_rows = block_rows.shape[2]
    low_rows = lax.slice_in_dim(low_all, 0, count_rows, axis=0)
    high_rows = lax.slice_in_dim(high_all, 0, count_rows, axis=0)
    apart_mask = no_shared(low_rows, high_rows, low_mine, high_mine).astype(jnp.bfloat16)
    order_sign = (
        jnp.sign(rank_mine[:, None, :] - hand_rank[:, :, None]).astype(jnp.bfloat16)
        * apart_mask[None]
    )
    showdown = zero_block + jnp.einsum(
        "blo,boh->blh", block_rows, order_sign, preferred_element_type=jnp.float32
    )
    folded = zero_block + jnp.einsum(
        "blo,oh->blh", block_rows, apart_mask, preferred_element_type=jnp.float32
    )
    showdown, folded = (showdown, folded)
    payoff = (
        jnp.where(kind_flat[:, :, None] == 1, showdown, folded)
        * stake_flat[:, :, None]
        * compat[:, None, :]
    )
    per_node = jnp.sum(payoff.reshape(boards_dev, actions_max, actions_max, hands_dev), axis=2)
    allowed = jnp.arange(actions_max)[None, :, None] < br_actions[:, None, None]
    sub_value = jnp.max(jnp.where(allowed, per_node, -1e30), axis=1)
    contrib = jax.ops.segment_sum(sub_value, root_parent, num_segments=node_total)
    last_mine = summed_on_arrival(contrib, LEAF, 0)
    whole_level = gather_directly(last_mine, LEAF, 0)
    level_list = [last_mine]
    for level_id in range(levels_count - 1, 0, -1):
        whole_level = jax.ops.segment_sum(
            whole_level, up_parent[level_id - 1], num_segments=node_total
        )
        level_list.insert(0, lax.dynamic_slice_in_dim(whole_level, node_start, nodes_dev))
    level_values = jnp.stack(level_list)
    local_total = jnp.sum(level_values[0], axis=0)
    root_value = of_everyone(local_total, LEAF) / node_total
    weighted_sum, range_total = lax.psum(
        (jnp.sum(br_range * root_value), jnp.sum(br_range)), "hand"
    )
    best_value = weighted_sum / range_total
    return (level_values, root_value, best_value)


def solution(mesh):
    split = Mesh(
        mesh.devices.reshape(8, 4, 2, mesh.shape["hand"]), ("leaf_0", "leaf_1", "leaf_2", "hand")
    )
    in_specs = (
        P("hand"),
        P("hand"),
        P(None, LEAF, "hand"),
        P(),
        P(LEAF, None),
        P(LEAF, None),
        P(LEAF),
        P(LEAF),
        P(LEAF, None),
        P(LEAF, None, None),
        P(LEAF, None, None),
        P(LEAF, None, None, "hand"),
    )
    out_specs = (P(None, LEAF, "hand"), P("hand"), P())
    return jax.shard_map(local, mesh=split, in_specs=in_specs, out_specs=out_specs, check_vma=False)
```

profile of v0, /device:TPU:1, one launch (start us, length us, event | category | flops | bytes accessed | tf_op | source)
XLA Modules:
  0.0 494.6 jit_solution(5926093371873539124)
XLA Ops:
  7.3 12.7 %all-gather = bf16[16,32,256]{2,1,0:T(8,128)(2,1)} all-gather(bf16[4,32,256]{2,1,0:T(8,128)(2,1)} %param.18), channel_id=2, replica_groups=mesh['leaf_0'=8,'leaf_1'=4,'leaf_2'=2,'hand'=4] {'leaf_1'}, dimensions={0}, use_global_device_ids=true | all-gather | bytes 327680 | tf_op jit(solution)/shard_map/all_gather | solution.py:23
  20.0 40.9 %all-gather.5.cloned.1.call-done = bf16[32,4,32,256]{3,2,1,0:T(8,128)(2,1)} async-done(((bf16[4,4,32,256]{3,2,1,0:T(8,128)(2,1)}), bf16[32,4,32,256]{3,2,1,0:T(8,128)(2,1)}) %all-gather.5.cloned.1.call-update) | async-done | bytes 2097168 | tf_op jit(solution)/shard_map/all_gather | solution.py:23
  68.3 16.9 %all-gather.7.cloned.1.call-done = bf16[64,4,32,256]{3,2,1,0:T(8,128)(2,1)} async-done(((bf16[32,4,32,256]{3,2,1,0:T(8,128)(2,1)}), bf16[64,4,32,256]{3,2,1,0:T(8,128)(2,1)}) %all-gather.7.cloned.1.call-update) | async-done | bytes 4194320 | tf_op jit(solution)/shard_map/all_gather | solution.py:23
  85.2 2.6 copy.32
  87.9 1.7 fusion.27
  89.8 9.3 %gather_fusion.1 = f32[2048,256]{1,0:T(8,128)} fusion(f32[2048,256]{1,0:T(8,128)S(1)} %convert_multiply_fusion.5, s32[2048]{0:T(1024)} %fusion.23), kind=kCustom, calls=%fused_computation.clone | custom fusion | bytes 4202496 | tf_op jit(solution)/shard_map/jit(_take)/gather | solution.py:121
  99.1 2.1 convert_multiply_fusion.4
  101.3 9.3 %gather_fusion.2 = f32[2048,256]{1,0:T(8,128)} fusion(f32[2048,256]{1,0:T(8,128)S(1)} %convert_multiply_fusion.4, s32[2048]{0:T(1024)} %fusion.24), kind=kCustom, calls=%fused_computation.1.clone | custom fusion | bytes 4202496 | tf_op jit(solution)/shard_map/jit(_take)/gather | solution.py:121
  110.5 2.1 convert_multiply_fusion.3
  112.7 9.3 %gather_fusion.3 = f32[2048,256]{1,0:T(8,128)} fusion(f32[2048,256]{1,0:T(8,128)S(1)} %convert_multiply_fusion.3, s32[2048]{0:T(1024)} %fusion.25), kind=kCustom, calls=%fused_computation.2.clone | custom fusion | bytes 4202496 | tf_op jit(solution)/shard_map/jit(_take)/gather | solution.py:121
  122.0 1.8 convert_multiply_fusion.2
  125.4 6.9 %fusion.9 = bf16[96,64,256]{2,1,0:T(8,128)(2,1)} fusion(f32[96,8,8]{2,1,0:T(8,128)S(1)} %fusion.22, bf16[96,8,8,256]{3,2,1,0:T(8,128)(2,1)} %param.27, f32[96,256]{1,0:T(8,128)S(1)} %get-tuple-element.19), kind=kOutput, calls=%fused_computation.20 | output fusion | flops 11206663 | bytes 6414336 | tf_op jit(solution)/shard_map/div | solution.py:129
  134.2 122.0 %all-gather.9.cloned.1.call-done = bf16[96,64,1024]{2,1,0:T(8,128)(2,1)} async-done(((bf16[96,64,256]{2,1,0:T(8,128)(2,1)}), bf16[96,64,1024]{2,1,0:T(8,128)(2,1)}) %all-gather.9.cloned.1.call-update) | async-done | bytes 12582928 | tf_op jit(solution)/shard_map/all_gather | solution.py:136
  256.3 8.5 %fusion.20 = f32[96,64,256]{2,1,0:T(8,128)S(1)} fusion(bf16[96,64,1024]{2,1,0:T(8,128)(2,1)} %all-gather.9.cloned.1.call-done, s32[256]{0:T(256)S(1)} %copy-done.9, s32[256]{0:T(256)S(1)} %copy-done.7, s32[1024]{0:T(1024)S(1)} %copy-done.11, s32[1024]{0:T(1024)S(1)} %copy-done.10), kind=kOutput, calls=%fused_computation.35 | convolution fusion | flops 3223584768 | bytes 18884608 | tf_op jit(solution)/shard_map/blo,oh->blh/dot_general | solution.py:148
  264.8 28.5 %bitcast_reduce_fusion = f32[96,8,256]{2,1,0:T(8,128)S(1)} fusion(f32[96,64,256]{2,1,0:T(8,128)S(1)} %fusion.20, f32[96,256]{1,0:T(8,128)S(1)} %get-tuple-element.18, f32[96,64]{1,0:T(8,128)S(1)} %copy.34, pred[96,64]{1,0:T(8,128)(4,1)S(1)} %copy.31, bf16[96,64,1024]{2,1,0:T(8,128)(2,1)S(1)} %copy-done.17, s32[96,1024]{1,0:T(8,128)S(1)} %copy-done.4, ...), kind=kOutput, calls=%fused_computation.15 | convolution fusion | flops 3327983616 | bytes 20805632 | tf_op jit(solution)/shard_map/blo,boh->blh/dot_general | solution.py:145
  295.3 62.1 %all_to_all.16 = f32[64,32,256]{2,1,0:T(8,128)} all-to-all(f32[64,32,256]{2,1,0:T(8,128)S(1)} %bitcast.47), channel_id=1, replica_groups=mesh['leaf_0'=8,'leaf_1'=4,'leaf_2'=2,'hand'=4] {'leaf_0','leaf_1','leaf..., dimensions={0} | all-to-all | bytes 4194304 | tf_op jit(solution)/shard_map/all_to_all | solution.py:41
  360.7 7.0 %all-to-all-start.1 = ((f32[64,32,256]{2,1,0:T(8,128)}), f32[64,32,256]{2,1,0:T(8,128)S(1)}, u32[]{:S(2)}, u32[]{:S(2)}) async-start(f32[64,32,256]{2,1,0:T(8,128)} %broadcast_in_dim.59), calls=%async_computation.1 | async-start | bytes 4194304 | tf_op jit(solution)/shard_map/all_to_all | solution.py:47
  367.7 49.7 %all-to-all-done.1 = f32[64,32,256]{2,1,0:T(8,128)S(1)} async-done(((f32[64,32,256]{2,1,0:T(8,128)}), f32[64,32,256]{2,1,0:T(8,128)S(1)}, u32[]{:S(2)}, u32[]{:S(2)}) %all-to-all-start.1) | async-done | bytes 2097184 | tf_op jit(solution)/shard_map/all_to_all | solution.py:47
  418.7 12.5 %scatter_custom_fusion.1 = f32[2048,256]{1,0:T(8,128)S(1)} fusion(s32[2048]{0:T(1024)} %bitcast.60, f32[2048,256]{1,0:T(8,128)} %bitcast.49, f32[]{:T(128)} %constant.20.clone.1), kind=kCustom, calls=%fused_computation.30 | custom fusion | flops 524288 | bytes 2097664 | tf_op jit(solution)/shard_map/scatter-add | solution.py:165
  431.2 13.0 %scatter_custom_fusion.2 = f32[2048,256]{1,0:T(8,128)} fusion(s32[2048]{0:T(1024)S(1)} %bitcast.57, f32[2048,256]{1,0:T(8,128)S(1)} %scatter_custom_fusion.1, f32[]{:T(128)} %constant.20.clone.1), kind=kCustom, calls=%fused_computation.28 | custom fusion | flops 524288 | bytes 2097156 | tf_op jit(solution)/shard_map/scatter-add | solution.py:165
  444.2 13.3 %scatter_custom_fusion.3 = f32[2048,256]{1,0:T(8,128)} fusion(s32[2048]{0:T(1024)S(1)} %bitcast.54, f32[2048,256]{1,0:T(8,128)} %scatter_custom_fusion.2, f32[]{:T(128)} %constant.20.clone.1), kind=kCustom, calls=%fused_computation.26 | custom fusion | flops 524288 | bytes 2097664 | tf_op jit(solution)/shard_map/scatter-add | solution.py:165
  459.0 7.0 %all-to-all-start.2 = ((f32[64,1,256]{2,1,0:T(1,128)}), f32[64,1,256]{2,1,0:T(1,128)S(1)}, u32[]{:S(2)}, u32[]{:S(2)}) async-start(f32[64,1,256]{2,1,0:T(1,128)} %broadcast_in_dim.96), calls=%async_computation.2 | async-start | bytes 131072 | tf_op jit(solution)/shard_map/all_to_all | solution.py:47
  467.4 8.6 %all-to-all-done.2 = f32[64,1,256]{2,1,0:T(1,128)S(1)} async-done(((f32[64,1,256]{2,1,0:T(1,128)}), f32[64,1,256]{2,1,0:T(1,128)S(1)}, u32[]{:S(2)}, u32[]{:S(2)}) %all-to-all-start.2) | async-done | bytes 65568 | tf_op jit(solution)/shard_map/all_to_all | solution.py:47
  477.3 8.4 %all-reduce = (f32[]{:T(128)}, f32[]{:T(128)}) all-reduce(f32[]{:T(128)} %get-tuple-element.5, f32[]{:T(128)} %get-tuple-element.4), channel_id=1, replica_groups=mesh['leaf_0'=8,'leaf_1'=4,'leaf_2'=2,'hand'=4] {'hand'}, use_global_device_ids=true, to_apply=%region_12.14 | all-reduce | flops 2 | bytes 16 | tf_op jit(solution)/shard_map/psum | solution.py:172
  (79 shorter events, 22.1 us)
Async XLA Ops:
  7.2 55.4 %copy-start.13 = (s32[96,8]{0,1:T(8,128)S(1)}, s32[96,8]{0,1:T(8,128)}, u32[]{:S(2)}) copy-start(s32[96,8]{0,1:T(8,128)} %param.24) | copy-start | bytes 9220
  7.2 55.4 %copy-start.18 = (s32[96]{0:T(128)S(1)}, s32[96]{0:T(128)}, u32[]{:S(2)}) copy-start(s32[96]{0:T(128)} %param.22) | copy-start | bytes 1156
  7.2 56.0 %copy-start.12 = (s32[96,5]{0,1:T(8,128)S(1)}, s32[96,5]{0,1:T(8,128)}, u32[]{:S(2)}) copy-start(s32[96,5]{0,1:T(8,128)} %param.20) | copy-start | bytes 5764
  7.2 57.4 %copy-start.5 = (s32[3,2048]{1,0:T(4,128)S(1)}, s32[3,2048]{1,0:T(4,128)}, u32[]{:S(2)}) copy-start(s32[3,2048]{1,0:T(4,128)} %param.19) | copy-start | bytes 73732
  7.2 53.7 %all-gather.5.cloned.1.call-start = ((), (), s32[]{:S(2)}) async-start(), calls=%async_computation.3 | async-start | bytes 2359296 | tf_op jit(solution)/shard_map/all_gather | solution.py:23
  19.9 65.3 %all-gather.7.cloned.1.call-start = ((), (), s32[]{:S(2)}) async-start(), calls=%async_computation.4 | async-start | bytes 6291456 | tf_op jit(solution)/shard_map/all_gather | solution.py:23
  60.9 195.3 %all-gather.9.cloned.1.call-start = ((), (), s32[]{:S(2)}) async-start(), calls=%async_computation.5 | async-start | bytes 15728640 | tf_op jit(solution)/shard_map/all_gather | solution.py:136
  61.8 2.3 copy-start.6
  62.5 1.5 copy-start.8
  64.6 23.3 %copy-start.1 = (s32[1,2048]{1,0:T(1,128)}, s32[1,2048]{1,0:T(1,128)S(1)}, u32[]{:S(2)}) copy-start(s32[1,2048]{1,0:T(1,128)S(1)} %get-tuple-element.15) | copy-start | bytes 24580
  87.9 1.8 copy-start.14
  132.3 0.8 copy-start.3
  132.3 0.9 copy-start.2
  132.3 1.0 copy-start.4
  132.3 1.0 copy-start.16
  132.3 1.1 copy-start.7
  132.4 1.1 copy-start.9
  132.4 1.1 copy-start.10
  132.4 1.1 copy-start.11
  256.3 8.5 %copy-start.17 = (bf16[96,64,1024]{2,1,0:T(8,128)(2,1)S(1)}, bf16[96,64,1024]{2,1,0:T(8,128)(2,1)}, u32[]{:S(2)}) copy-start(bf16[96,64,1024]{2,1,0:T(8,128)(2,1)} %all-gather.9.cloned.1.call-done) | copy-start | bytes 37748740
  360.7 56.7 %all-to-all-start.1 = ((f32[64,32,256]{2,1,0:T(8,128)}), f32[64,32,256]{2,1,0:T(8,128)S(1)}, u32[]{:S(2)}, u32[]{:S(2)}) async-start(f32[64,32,256]{2,1,0:T(8,128)} %broadcast_in_dim.59), calls=%async_computation.1 | async-start | bytes 4194304 | tf_op jit(solution)/shard_map/all_to_all | solution.py:47
  417.4 1.4 copy-start
  431.2 44.9 %copy-start.15 = (f32[256]{0:T(256)S(1)}, f32[256]{0:T(256)}, u32[]{:S(2)}) copy-start(f32[256]{0:T(256)} %param.17) | copy-start | bytes 3076
  459.0 17.0 %all-to-all-start.2 = ((f32[64,1,256]{2,1,0:T(1,128)}), f32[64,1,256]{2,1,0:T(1,128)S(1)}, u32[]{:S(2)}, u32[]{:S(2)}) async-start(f32[64,1,256]{2,1,0:T(1,128)} %broadcast_in_dim.96), calls=%async_computation.2 | async-start | bytes 131072 | tf_op jit(solution)/shard_map/all_to_all | solution.py:47
Sparse Core Ops, SparseCore 0:
  20.1 40.8 all-gather.4
  62.7 22.4 all-gather.6
  132.5 123.6 all-gather.8
where the time goes:
time: 496 us; the launch traced here: 495 us
  waiting for transfers between devices  238 us (48%)
  blocking collectives  83.1 us (17%)
  other arithmetic  65.8 us (13%)
  local copies, waits for them, and re-layouts  40.1 us (8%)
  matrix products  37 us (7%)
  between operations  16.5 us (3%)
  starting transfers between devices  14 us (3%)
    all_gather x1, waiting for transfers between devices, local(): block_rows = lax.all_gather(leaf_reach, 'hand', axis=2, tiled=True)  122 us
    all_to_all x1, blocking collectives, summed_on_arrival(): lax.all_to_all(parts, axis, split_axis=0, concat_axis=0, tiled=True)  62.1 us
    all_to_all x2, waiting for transfers between devices, copy_for_each(): lax.all_to_all(jnp.broadcast_to(x[None], (devices, *x.shape)), axis, 0, 0...  58.3 us
    all_gather x2, waiting for transfers between devices, all_blocks(): parts = lax.all_gather(parts, axes[k], axis=0, tiled=True)  57.8 us
    scatter-add x3, other arithmetic, local(): jax.ops.segment_sum(whole_level, up_parent[level_id - 1], num_segments=no...  38.8 us
    dot_general x1, matrix products, local(): jnp.einsum('blo,boh->blh', block_rows, order_sign, preferred_element_type...  28.5 us
    gather x3, local copies, waits for them, and re-layouts, local(): jnp.take(gathered, up_parent[level_id - 1], axis=0)  27.9 us
    all_to_all x2, starting transfers between devices, copy_for_each(): lax.all_to_all(jnp.broadcast_to(x[None], (devices, *x.shape)), axis, 0, 0...  13.9 us
  transfers between devices with their start and end apart: 5, of which 5 were waited for; matrix products, arithmetic and copies ran while one was open for 2% of the time, Pallas kernels for 0%

commit v1 on v0

v1 whole, which is shorter than its diff:
```python
import functools

import jax
import jax.numpy as jnp
import numpy as np
from jax import lax
from jax.experimental import pallas as pl
from jax.experimental.pallas import tpu as pltpu
from jax.sharding import PartitionSpec as P

MESH = pl.DeviceIdType.MESH
F32 = jnp.float32
BF16 = jnp.bfloat16
PAYOFF_UNIT = 1.0 / 4096.0
VMEM = pltpu.VMEM


def vmem_specs(number):
    return [pl.BlockSpec(memory_space=VMEM)] * number


def exchange_kernel(axis, n, x_ref, o_ref, send_sem, recv_sem, own_sem):
    me = lax.axis_index(axis)
    barrier = pltpu.get_barrier_semaphore()

    def greet(i, carry):
        pl.semaphore_signal(
            barrier, inc=1, device_id={axis: lax.rem(me + i, n)}, device_id_type=MESH
        )
        return carry

    lax.fori_loop(1, n, greet, 0)
    own = pltpu.make_async_copy(x_ref.at[me], o_ref.at[me], own_sem)
    own.start()
    pl.semaphore_wait(barrier, n - 1)

    def send(i, carry):
        peer = lax.rem(me + i, n)
        pltpu.make_async_remote_copy(
            src_ref=x_ref.at[peer],
            dst_ref=o_ref.at[me],
            send_sem=send_sem,
            recv_sem=recv_sem,
            device_id={axis: peer},
            device_id_type=MESH,
        ).start()
        return carry

    lax.fori_loop(1, n, send, 0)
    own.wait()
    others = pl.ds(0, n - 1)
    pltpu.make_async_copy(o_ref.at[others], o_ref.at[others], recv_sem).wait()
    pltpu.make_async_copy(x_ref.at[others], x_ref.at[others], send_sem).wait()


def exchange(x, axis, cid):
    n = x.shape[0]
    return pl.pallas_call(
        functools.partial(exchange_kernel, axis, n),
        out_shape=jax.ShapeDtypeStruct(x.shape, x.dtype),
        in_specs=vmem_specs(1),
        out_specs=pl.BlockSpec(memory_space=VMEM),
        scratch_shapes=[pltpu.SemaphoreType.DMA] * 3,
        compiler_params=pltpu.CompilerParams(collective_id=cid, has_side_effects=True),
        name=f"exchange_{cid}",
    )(x)


def lane_take(table, lanes):
    return jnp.take_along_axis(table, lanes, axis=1, mode="promise_in_bounds")


def look_up(first, second, index):
    lanes = index & 127
    tile = index >> 7
    out = jnp.zeros(index.shape, F32)
    for m in range(8):
        out = jnp.where(tile == m, lane_take(first[m], lanes), out)
        out = jnp.where(tile == m + 8, lane_take(second[m], lanes), out)
    return out


def reach_kernel(w_ref, parent_ref, opp_ref, root_ref, out_ref, now_ref):
    low_half = lax.broadcasted_iota(jnp.int32, (8, 128), 0) < 4

    def tables():
        first, second = [], []
        for m in range(8):
            here = now_ref[:, m * 128 : (m + 1) * 128]
            swapped = pltpu.roll(here, 4, 0)
            first.append(jnp.where(low_half, here, swapped))
            second.append(jnp.where(low_half, swapped, here))
        return first, second

    for m in range(8):
        cut = slice(m * 128, (m + 1) * 128)
        now_ref[:, cut] = w_ref[0, :, cut] * opp_ref[...]
    for level in range(1, 4):
        first, second = tables()
        for m in range(8):
            cut = slice(m * 128, (m + 1) * 128)
            now_ref[:, cut] = (
                look_up(first, second, parent_ref[level - 1, :, cut]) * w_ref[level, :, cut]
            )
    first, second = tables()

    def one(i, carry):
        out_ref[i] = look_up(first, second, root_ref[i])
        return carry

    lax.fori_loop(0, root_ref.shape[0], one, 0)


def leaf_kernel(w_ref, root_ref, flat_ref, out_ref):
    rows, act2, hands = w_ref.shape
    act = act2 // 8
    own_block = lax.broadcasted_iota(jnp.int32, (act, act2), 1) // act == lax.broadcasted_iota(
        jnp.int32, (act, act2), 0
    )
    for s in range(rows):
        flats = flat_ref[s]
        spread = [
            jnp.where(own_block, jnp.broadcast_to(flats[i : i + 1], (act, act2)), 0.0)
            for i in range(5)
        ]
        coef = jnp.concatenate(spread[:4], axis=0).astype(BF16)
        w = w_ref[s]
        total = jnp.dot(spread[4].astype(BF16), w, preferred_element_type=F32)
        factor = root_ref[s : s + 1, :] / total
        wide = w.astype(F32).reshape(act, act, hands) * factor[:, None, :]
        reach = wide.reshape(act2, hands).astype(BF16)
        y = jnp.dot(coef, reach, preferred_element_type=F32)
        y1 = y[0:8] + y[8:16]
        y0 = y[16:24] + y[24:32]
        high1 = y1.astype(BF16).astype(F32)
        high0 = y0.astype(BF16).astype(F32)
        out_ref[s, 0:16, :] = jnp.concatenate([high1, y1 - high1], axis=0).astype(BF16)
        out_ref[s, 16:32, :] = jnp.concatenate([high0, y0 - high0], axis=0).astype(BF16)


def board_kernel(
    br_ref, y_ref, row_ref, col_ref, compat_ref, card_row_ref, card_col_ref, out_ref, apart, minus, sign
):
    group = pl.program_id(0)
    parts, _, _, depth = y_ref.shape
    hands = row_ref.shape[1]

    @pl.when(group == 0)
    def _():
        low_r, high_r = card_row_ref[0:1, :], card_row_ref[1:2, :]

        def strip(i, carry):
            rows = pl.ds(pl.multiple_of(i * 16, 16), 16)
            low_c = jnp.broadcast_to(card_col_ref[rows, 0:1], (16, hands))
            high_c = jnp.broadcast_to(card_col_ref[rows, 1:2], (16, hands))
            share = (low_c == low_r) | (low_c == high_r) | (high_c == low_r) | (high_c == high_r)
            keep = jnp.where(share, 0.0, 1.0)
            apart[rows, :] = keep.astype(BF16)
            minus[rows, :] = (0.0 - keep).astype(BF16)
            return carry

        lax.fori_loop(0, hands // 16, strip, 0)

    folded = jnp.zeros((128, hands), F32)
    for q in range(parts):
        low_rows = y_ref[q, :, 16:32, :].reshape(128, depth)
        folded += jnp.dot(
            low_rows, apart[q * depth : (q + 1) * depth, :], preferred_element_type=F32
        )
    act_row = lax.broadcasted_iota(jnp.int32, (8, hands), 0)
    for s in range(8):
        total = jnp.zeros((16, hands), F32)
        mine = row_ref[s : s + 1, :]
        for q in range(parts):
            slot = (s * parts + q) % 2
            for strip in range(depth // 16):
                at = q * depth + strip * 16
                gap = mine - col_ref[0, at : at + 16, s : s + 1]
                near = gap.astype(BF16)
                sign[slot, strip * 16 : strip * 16 + 16, :] = jnp.maximum(
                    jnp.minimum(near, apart[at : at + 16, :]), minus[at : at + 16, :]
                )
            total += jnp.dot(y_ref[q, s, 0:16, :], sign[slot], preferred_element_type=F32)
        node = total[0:8] + total[8:16] + folded[s * 16 : s * 16 + 8] + folded[s * 16 + 8 : s * 16 + 16]
        node = node * PAYOFF_UNIT * compat_ref[s : s + 1, :]
        node = jnp.where(act_row < br_ref[group * 8 + s], node, -1e30)
        out_ref[s : s + 1, :] = jnp.max(node, axis=0, keepdims=True)


def sums_kernel(v_ref, root_ref, parent_ref, out_ref, total_ref, now_ref):
    sub_row = lax.broadcasted_iota(jnp.int32, (8, 128), 0)
    upper = sub_row // 4
    lane_row = lax.broadcasted_iota(jnp.int32, (128, 128), 0)

    def block(values, index, acc):
        twice = jnp.concatenate([values, values], axis=0)
        high = twice.astype(BF16).astype(F32)
        low = twice - high
        big = jnp.broadcast_to(index >> 7, (8, 128))
        picked_high = [jnp.where(big == 2 * i + upper, high, 0.0) for i in range(8)]
        picked_low = [jnp.where(big == 2 * i + upper, low, 0.0) for i in range(8)]
        left = jnp.concatenate(picked_high + picked_low, axis=0).astype(BF16)
        right = jnp.where(jnp.broadcast_to(index & 127, (128, 128)) == lane_row, 1.0, 0.0).astype(BF16)
        return acc + lax.dot_general(
            left, right, (((1,), (1,)), ((), ())), preferred_element_type=F32
        )

    def from_boards(i, acc):
        return block(v_ref[i], root_ref[pl.ds(i, 1), :], acc)

    acc = lax.fori_loop(0, v_ref.shape[0], from_boards, jnp.zeros((128, 128), F32))
    levels = [None] * 4
    for level in range(3, -1, -1):
        levels[level] = acc[0:64] + acc[64:128]
        if level > 0:
            acc = jnp.zeros((128, 128), F32)
            for t in range(16):
                acc = block(
                    levels[level][4 * t : 4 * t + 4], parent_ref[level - 1, t : t + 1, :], acc
                )
    place = lax.broadcasted_iota(jnp.int32, (64, 128), 1) // 32
    for q in range(4):
        out = jnp.zeros((64, 128), F32)
        for level in range(4):
            shift = ((level - q) * 32) % 128
            moved = levels[level] if shift == 0 else pltpu.roll(levels[level], shift, 1)
            out = jnp.where(place == level, moved, out)
        out_ref[q] = out
    total_ref[...] = levels[0]


def hand_cards(number):
    low_list = []
    high_list = []
    for low_card in range(52):
        for high_card in range(low_card + 1, 52):
            low_list.append(low_card)
            high_list.append(high_card)
    chosen = np.arange(number) * 1326 // number
    return (np.array(low_list, np.int32)[chosen], np.array(high_list, np.int32)[chosen])


def board_compat(board_cards, low_cols, high_cols):
    hits = (board_cards[:, :, None] == low_cols[None, None, :]) | (
        board_cards[:, :, None] == high_cols[None, None, :]
    )
    return 1.0 - jnp.any(hits, axis=1).astype(F32)


def local(
    opp_range,
    br_range,
    up_weight,
    up_parent,
    board_cards,
    hand_rank,
    root_parent,
    br_actions,
    opp_actions,
    leaf_kind,
    leaf_stake,
    opp_weight,
):
    leaf_at = lax.axis_index("leaf")
    hand_at = lax.axis_index("hand")
    low_np, high_np = hand_cards(1024)
    low_all, high_all = jnp.asarray(low_np), jnp.asarray(high_np)
    low_mine = lax.dynamic_slice_in_dim(low_all, hand_at * 256, 256)
    high_mine = lax.dynamic_slice_in_dim(high_all, hand_at * 256, 256)

    out1 = up_weight.astype(F32).reshape(128, 256).T.reshape(64, 4, 128)
    parents = jnp.pad(root_parent.astype(F32), (0, 32))
    out1 = jnp.concatenate([out1, jnp.broadcast_to(parents, (64, 1, 128))], axis=1)
    got1 = exchange(out1, "leaf", 0)
    weights = got1[:, :4].reshape(32 * 2, 4, 4, 32).transpose(2, 1, 0, 3).reshape(4, 4, 2, 1024)
    weights = weights.transpose(0, 2, 1, 3).reshape(4, 8, 1024)
    roots = got1[:, 4].astype(jnp.int32)
    root_index = jnp.broadcast_to(roots[:, None, :], (64, 4, 128)).reshape(32, 8, 128)
    parent_index = jnp.broadcast_to(up_parent.reshape(3, 2, 1, 1024), (3, 2, 4, 1024)).reshape(3, 8, 1024)
    opp4 = lax.dynamic_slice_in_dim(opp_range, leaf_at * 4, 4)
    opp8 = jnp.broadcast_to(jnp.concatenate([opp4, opp4])[:, None], (8, 128))
    out2 = pl.pallas_call(
        reach_kernel,
        out_shape=jax.ShapeDtypeStruct((32, 8, 128), F32),
        in_specs=vmem_specs(4),
        out_specs=pl.BlockSpec(memory_space=VMEM),
        scratch_shapes=[VMEM((8, 1024), F32)],
        name="reach",
    )(weights, parent_index, opp8, root_index)
    got2 = exchange(out2.reshape(64, 4, 128), "leaf", 1)
    compat = board_compat(board_cards, low_mine, high_mine)
    root_reach = got2.reshape(256, 128).T[:96] * compat

    legal = (jnp.arange(8)[None, None, :] < opp_actions[:, :, None]).astype(jnp.int32)
    shown = (leaf_kind == 1).astype(jnp.int32) * leaf_stake * legal
    fold = (leaf_kind != 1).astype(jnp.int32) * leaf_stake * legal
    flats = jnp.stack(
        [shown & ~15, shown & 15, fold & ~15, fold & 15, legal, legal, legal, legal], axis=1
    )
    flats = flats.reshape(96, 8, 64).astype(F32)
    weights_flat = opp_weight.reshape(96, 64, 256)
    y = pl.pallas_call(
        leaf_kernel,
        grid=(12,),
        out_shape=jax.ShapeDtypeStruct((96, 32, 256), BF16),
        in_specs=[
            pl.BlockSpec((8, 64, 256), lambda i: (i, 0, 0)),
            pl.BlockSpec((8, 256), lambda i: (i, 0)),
            pl.BlockSpec((8, 8, 64), lambda i: (i, 0, 0)),
        ],
        out_specs=pl.BlockSpec((8, 32, 256), lambda i: (i, 0, 0)),
        name="leaf",
    )(weights_flat, root_reach, flats)
    y_all = exchange(y.reshape(4, 24, 32, 256), "hand", 2)

    ranks = lax.dynamic_slice_in_dim(hand_rank, hand_at * 24, 24).astype(F32)
    boards = lax.dynamic_slice_in_dim(board_cards, hand_at * 24, 24)
    br_mine = lax.dynamic_slice_in_dim(br_actions, hand_at * 24, 24)
    compat_all = board_compat(boards, low_all, high_all)
    columns = ranks.reshape(3, 8, 1024).transpose(0, 2, 1)
    cards = jnp.stack([low_all, high_all]).astype(F32)
    sub = pl.pallas_call(
        board_kernel,
        grid_spec=pltpu.PrefetchScalarGridSpec(
            num_scalar_prefetch=1,
            grid=(3,),
            in_specs=[
                pl.BlockSpec((4, 8, 32, 256), lambda i, br: (0, i, 0, 0)),
                pl.BlockSpec((8, 1024), lambda i, br: (i, 0)),
                pl.BlockSpec((1, 1024, 8), lambda i, br: (i, 0, 0)),
                pl.BlockSpec((8, 1024), lambda i, br: (i, 0)),
                pl.BlockSpec((2, 1024), lambda i, br: (0, 0)),
                pl.BlockSpec((1024, 2), lambda i, br: (0, 0)),
            ],
            out_specs=pl.BlockSpec((8, 1024), lambda i, br: (i, 0)),
            scratch_shapes=[
                VMEM((1024, 1024), BF16),
                VMEM((1024, 1024), BF16),
                VMEM((2, 256, 1024), BF16),
            ],
        ),
        out_shape=jax.ShapeDtypeStruct((24, 1024), F32),
        name="boards",
    )(br_mine, y_all, ranks, columns, compat_all, cards, cards.T)
    sub_value = exchange(sub.reshape(24, 4, 256).transpose(1, 0, 2), "hand", 3).reshape(96, 256)

    out3 = jnp.pad(sub_value.T, ((0, 0), (0, 32))).reshape(64, 4, 128)
    got3 = exchange(out3, "leaf", 4)
    level_out, totals = pl.pallas_call(
        sums_kernel,
        out_shape=(
            jax.ShapeDtypeStruct((4, 64, 128), F32),
            jax.ShapeDtypeStruct((64, 128), F32),
        ),
        in_specs=vmem_specs(3),
        out_specs=(pl.BlockSpec(memory_space=VMEM), pl.BlockSpec(memory_space=VMEM)),
        scratch_shapes=[VMEM((8, 128), F32)],
        name="sums",
    )(got3, roots, up_parent.reshape(3, 16, 128))
    root4 = jnp.sum(totals.reshape(16, 4, 128), axis=(0, 2))
    out4 = level_out.reshape(4, 16, 4, 128).transpose(1, 0, 2, 3).reshape(64, 4, 128)
    root_row = jnp.broadcast_to(jnp.pad(root4, (0, 124)), (64, 1, 128))
    got4 = exchange(jnp.concatenate([out4, root_row], axis=1), "leaf", 5)
    level_values = got4[:, :4].reshape(256, 128).T.reshape(4, 32, 256)
    root_value = got4[:, 4, :4].reshape(256) / 2048
    pair = jnp.stack([jnp.sum(br_range * root_value), jnp.sum(br_range)])
    pair = jnp.broadcast_to(jnp.pad(pair, (0, 126)), (4, 8, 128))
    both = exchange(pair, "hand", 6)
    both = jnp.sum(both[:, 0], axis=0)
    return level_values, root_value, both[0] / both[1]


def solution(mesh):
    in_specs = (
        P("hand"),
        P("hand"),
        P(None, "leaf", "hand"),
        P(),
        P("leaf", None),
        P("leaf", None),
        P("leaf"),
        P("leaf"),
        P("leaf", None),
        P("leaf", None, None),
        P("leaf", None, None),
        P("leaf", None, None, "hand"),
    )
    out_specs = (P(None, "leaf", "hand"), P("hand"), P())
    return jax.shard_map(local, mesh=mesh, in_specs=in_specs, out_specs=out_specs, check_vma=False)
```

time: 496 us -> 185 us (0.37)
  waiting for transfers between devices: 238 us -> 0 us
  Pallas kernels: 0 us -> 148 us
  blocking collectives: 83.1 us -> 0 us
  other arithmetic: 65.8 us -> 11.6 us
  matrix products: 37 us -> 0 us
  local copies, waits for them, and re-layouts: 40.1 us -> 20.2 us
  starting transfers between devices: 14 us -> 0 us
  between operations: 16.5 us -> 3.48 us
    all_gather x3 -> x0, waiting for transfers between devices: 180 us -> none  [the longest x1 122 us: local(): block_rows = lax.all_gather(leaf_reach, 'hand', axis=2, tiled=True)]
    pallas_call x0 -> x11, Pallas kernels: none -> 148 us  [the longest x7 97.8 us: exchange(): pl.pallas_call(functools.partial(exchange_kernel, axis, n), out_shape=jax...]
    all_to_all x1 -> x0, blocking collectives: 62.1 us -> none  [summed_on_arrival(): lax.all_to_all(parts, axis, split_axis=0, concat_axis=0, tiled=True)]
    all_to_all x2 -> x0, waiting for transfers between devices: 58.3 us -> none  [copy_for_each(): lax.all_to_all(jnp.broadcast_to(x[None], (devices, *x.shape)), axis, 0, 0...]
    scatter-add x4 -> x0, other arithmetic: 40.5 us -> none  [the longest x3 38.8 us: local(): jax.ops.segment_sum(whole_level, up_parent[level_id - 1], num_segments=no...]
    dot_general x2 -> x0, matrix products: 37 us -> none  [the longest x1 28.5 us: local(): jnp.einsum('blo,boh->blh', block_rows, order_sign, preferred_element_type...]
    gather x4 -> x0, local copies, waits for them, and re-layouts: 28.7 us -> none  [the longest x3 27.9 us: local(): jnp.take(gathered, up_parent[level_id - 1], axis=0)]
    all_to_all x2 -> x0, starting transfers between devices: 13.9 us -> none  [copy_for_each(): lax.all_to_all(jnp.broadcast_to(x[None], (devices, *x.shape)), axis, 0, 0...]
  transfers between devices with their start and end apart: 5 -> 0, of which waited for: 5 -> 0; matrix products, arithmetic and copies ran while one was open for 2% -> 0% of each run, Pallas kernels for 0% -> 0%
where the time goes in v1:
time: 185 us; the launch traced here: 184 us
  Pallas kernels  148 us (80%)
  local copies, waits for them, and re-layouts  20.2 us (11%)
  other arithmetic  11.6 us (6%)
  between operations  3.48 us (2%)
    pallas_call x7, Pallas kernels, exchange(): pl.pallas_call(functools.partial(exchange_kernel, axis, n), out_shape=jax...  97.8 us
    pallas_call x1, Pallas kernels, local(): pl.pallas_call(board_kernel, grid_spec=pltpu.PrefetchScalarGridSpec(num_s...  22.2 us
    pallas_call x1, Pallas kernels, local(): pl.pallas_call(sums_kernel, out_shape=(jax.ShapeDtypeStruct((4, 64, 128),...  13.7 us
    pallas_call x1, Pallas kernels, local(): pl.pallas_call(leaf_kernel, grid=(12,), out_shape=jax.ShapeDtypeStruct((9...  9.53 us
    pallas_call x1, Pallas kernels, local(): pl.pallas_call(reach_kernel, out_shape=jax.ShapeDtypeStruct((32, 8, 128),...  5.15 us

profile of v1, /device:TPU:1, one launch (start us, length us, event | category | flops | bytes accessed | tf_op | source)
XLA Modules:
  0.0 183.7 jit_solution(11842185912551734135)
XLA Ops:
  2.2 0.9 or_reduce_fusion.1
  4.5 0.8 bitcast_convert_fusion
  6.9 19.0 %exchange_0.1 = f32[64,5,128]{2,1,0:T(8,128)} custom-call(f32[64,5,128]{2,1,0:T(8,128)} %pad_maximum_fusion.x_ref), custom_call_target="tpu_custom_call" | custom-call | tf_op jit(solution)/shard_map/exchange_0/pallas_call | solution.py:58
  26.0 1.0 slice.25
  27.7 1.0 slice.24
  30.8 5.2 %reach.1 = f32[32,8,128]{2,1,0:T(8,128)} custom-call(f32[4,8,1024]{2,1,0:T(8,128)} %reshape.154.w_ref, s32[3,8,1024]{2,1,0:T(8,128)} %reshape.155.parent_ref, f32[8,128]{1,0:T(8,128)} %broadcast_in_dim.19.opp_ref, s32[32,8,128]{2,1,0:T(8,128)} %bitcast.65), custom_call_target="tpu_custom_call" | custom-call | tf_op jit(solution)/shard_map/reach/pallas_call | solution.py:282
  36.0 13.4 %exchange_1.1 = f32[64,4,128]{2,1,0:T(4,128)} custom-call(f32[64,4,128]{2,1,0:T(4,128)} %bitcast.71), custom_call_target="tpu_custom_call" | custom-call | tf_op jit(solution)/shard_map/exchange_1/pallas_call | solution.py:58
  49.4 1.0 copy.69
  53.1 9.5 %leaf.1 = bf16[96,32,256]{2,1,0:T(8,128)(2,1)} custom-call(bf16[96,64,256]{2,1,0:T(8,128)(2,1)} %bitcast.61, f32[96,256]{1,0:T(8,128)} %slice_multiply_fusion.root_ref, f32[96,8,64]{2,1,0:T(8,128)} %convert_element_type.50.flat_ref), custom_call_target="tpu_custom_call" | custom-call | tf_op jit(solution)/shard_map/leaf/pallas_call | solution.py:302
  62.7 23.5 %exchange_2.1.y_ref = bf16[4,24,32,256]{3,2,1,0:T(8,128)(2,1)} custom-call(bf16[4,24,32,256]{3,2,1,0:T(8,128)(2,1)} %bitcast.60), custom_call_target="tpu_custom_call" | custom-call | tf_op jit(solution)/shard_map/exchange_2/pallas_call | solution.py:58
  86.3 1.6 copy.76
  90.1 22.2 %boards.1 = f32[24,1024]{1,0:T(8,128)} custom-call(s32[24]{0:T(128)} %dynamic_slice.18.br_ref, bf16[4,24,32,256]{3,2,1,0:T(8,128)(2,1)} %exchange_2.1.y_ref, f32[24,1024]{1,0:T(8,128)} %dynamic-slice_convert_fusion.row_ref, f32[3,1024,8]{2,1,0:T(8,128)} %bitcast.59, f32[24,1024]{1,0:T(8,128)} %convert_subtract_fusion.compat_ref, ...), custom_call_target="tpu_custom_call" | custom-call | tf_op jit(solution)/shard_map/boards/pallas_call | solution.py:322
  112.3 1.6 copy.86
  113.9 6.7 %exchange_3.1 = f32[4,24,256]{2,1,0:T(8,128)} custom-call(f32[4,24,256]{2,1,0:T(8,128)} %bitcast.73), custom_call_target="tpu_custom_call" | custom-call | tf_op jit(solution)/shard_map/exchange_3/pallas_call | solution.py:58
  120.6 1.0 copy.78
  122.2 15.2 %exchange_4.1.v_ref = f32[64,4,128]{2,1,0:T(4,128)} custom-call(f32[64,4,128]{2,1,0:T(4,128)} %bitcast.69), custom_call_target="tpu_custom_call" | custom-call | tf_op jit(solution)/shard_map/exchange_4/pallas_call | solution.py:58
  138.0 13.7 %sums.1 = (f32[4,64,128]{2,1,0:T(8,128)}, f32[64,128]{1,0:T(8,128)}) custom-call(f32[64,4,128]{2,1,0:T(4,128)} %exchange_4.1.v_ref, s32[64,128]{1,0:T(8,128)} %copy-done, s32[3,16,128]{2,1,0:T(8,128)} %bitcast.80), custom_call_target="tpu_custom_call" | custom-call | tf_op jit(solution)/shard_map/sums/pallas_call | solution.py:349
  151.7 0.9 copy.79
  152.6 0.9 reduce_sum.43
  154.4 14.6 %exchange_5.1 = f32[64,5,128]{2,1,0:T(8,128)} custom-call(f32[64,5,128]{2,1,0:T(8,128)} %pad_maximum_fusion.1.x_ref), custom_call_target="tpu_custom_call" | custom-call | tf_op jit(solution)/shard_map/exchange_5/pallas_call | solution.py:58
  169.1 1.1 multiply_reduce_fusion
  170.8 1.4 fusion
  172.8 5.3 %exchange_6.1 = f32[4,8,128]{2,1,0:T(8,128)} custom-call(f32[4,8,128]{2,1,0:T(8,128)} %broadcast_in_dim.23.x_ref), custom_call_target="tpu_custom_call" | custom-call | tf_op jit(solution)/shard_map/exchange_6/pallas_call | solution.py:58
  180.8 1.0 slice.27
  (75 shorter events, 17.8 us)
Async XLA Ops:
  25.9 4.2 %copy-start.1 = (s32[3,2048]{1,0:T(4,128)S(1)}, s32[3,2048]{1,0:T(4,128)}, u32[]{:S(2)}) copy-start(s32[3,2048]{1,0:T(4,128)} %param.17) | copy-start | bytes 73732
  27.0 3.9 %copy-start = (s32[64,128]{1,0:T(8,128)}, s32[64,128]{1,0:T(8,128)S(1)}, u32[]{:S(2)}) copy-start(s32[64,128]{1,0:T(8,128)S(1)} %convert_bitcast_fusion.root_ref) | copy-start | bytes 98308
  29.0 22.1 %copy-start.3 = (s32[96,8,8]{0,2,1:T(8,128)S(1)}, s32[96,8,8]{0,2,1:T(8,128)}, u32[]{:S(2)}) copy-start(s32[96,8,8]{0,2,1:T(8,128)} %param.24) | copy-start | bytes 73732
  29.0 22.1 %copy-start.4 = (s32[96,8,8]{0,2,1:T(8,128)S(1)}, s32[96,8,8]{0,2,1:T(8,128)}, u32[]{:S(2)}) copy-start(s32[96,8,8]{0,2,1:T(8,128)} %param.23) | copy-start | bytes 73732
  29.0 22.1 %copy-start.8 = (s32[96,8]{0,1:T(8,128)S(1)}, s32[96,8]{0,1:T(8,128)}, u32[]{:S(2)}) copy-start(s32[96,8]{0,1:T(8,128)} %param.22) | copy-start | bytes 9220
  62.7 23.6 %copy-start.2 = (s32[96,1024]{1,0:T(8,128)S(1)}, s32[96,1024]{1,0:T(8,128)}, u32[]{:S(2)}) copy-start(s32[96,1024]{1,0:T(8,128)} %param.19) | copy-start | bytes 1179652
  86.2 1.7 copy-start.5
  86.2 1.8 copy-start.6
  86.2 1.8 copy-start.7
  86.2 3.2 %copy-start.11 = (s32[96]{0:T(128)S(1)}, s32[96]{0:T(128)}, u32[]{:S(2)}) copy-start(s32[96]{0:T(128)} %param.21) | copy-start | bytes 1156
  112.3 57.9 %copy-start.10 = (f32[256]{0:T(256)S(1)}, f32[256]{0:T(256)}, u32[]{:S(2)}) copy-start(f32[256]{0:T(256)} %param.15) | copy-start | bytes 3076
  170.2 12.3 %copy-start.9 = (f32[256]{0:T(256)}, f32[256]{0:T(256)S(1)}, u32[]{:S(2)}) copy-start(f32[256]{0:T(256)S(1)} %div.16) | copy-start | bytes 3076

commit v2 on v0

v2 whole, which is shorter than its diff:
```python
import jax
import jax.numpy as jnp
import numpy as np
from jax import lax
from jax.experimental import pallas as pl
from jax.experimental.pallas import tpu as pltpu
from jax.sharding import PartitionSpec as P

MESH = pl.DeviceIdType.MESH
F32 = jnp.float32
BF16 = jnp.bfloat16
I32 = jnp.int32
PAYOFF_UNIT = 1.0 / 4096.0
VMEM = pltpu.VMEM
LEAVES = 64
SIDES = 4


def dot(a, b):
    return jnp.dot(a, b, preferred_element_type=F32)


def dot_t(a, b):
    return lax.dot_general(a, b, (((1,), (1,)), ((), ())), preferred_element_type=F32)


def lane_take(table, lanes):
    return jnp.take_along_axis(table, lanes, axis=1, mode="promise_in_bounds")


def look_up(first, second, index):
    lanes = index & 127
    tile = index >> 7
    parts = []
    for m in range(8):
        parts.append(jnp.where(tile == m, lane_take(first[m], lanes), 0.0))
        parts.append(jnp.where(tile == m + 8, lane_take(second[m], lanes), 0.0))
    while len(parts) > 1:
        parts = [parts[i] + parts[i + 1] for i in range(0, len(parts), 2)]
    return parts[0]


def card_hits(card, low, high):
    return (card == low) | (card == high)


def kernel(
    br_act,
    up_ref,
    root_ref,
    parent_ref,
    opp_ref,
    br_ref,
    cards_ref,
    card_col_ref,
    board_ref,
    rank_ref,
    code_ref,
    w_hbm,
    level_ref,
    value_ref,
    best_ref,
    w_ref,
    apart,
    minus,
    sign,
    s1,
    r1,
    s2,
    r2,
    s3,
    r3,
    s4,
    r4,
    sy,
    ry,
    sx,
    rx,
    br_all,
    weights,
    now_ref,
    turned,
    board_sum,
    reach_ref,
    inverse,
    column,
    node_ref,
    compat_all,
    sub_ref,
    left,
    right,
    right_up,
    leaf_send,
    leaf_recv,
    own_sem,
    w_sem,
    y_send,
    y_recv,
    x_send,
    x_recv,
    b_send,
    b_recv,
):
    leaf_at = lax.axis_index("leaf")
    hand_at = lax.axis_index("hand")
    barrier = pltpu.get_barrier_semaphore()

    def greet_leaf(i, carry):
        pl.semaphore_signal(
            barrier, inc=1, device_id={"leaf": lax.rem(leaf_at + i, LEAVES)}, device_id_type=MESH
        )
        return carry

    lax.fori_loop(1, LEAVES, greet_leaf, 0)
    for i in range(1, SIDES):
        pl.semaphore_signal(
            barrier, inc=1, device_id={"hand": lax.rem(hand_at + i, SIDES)}, device_id_type=MESH
        )
    w_copy = pltpu.make_async_copy(w_hbm, w_ref, w_sem)
    w_copy.start()

    def leaf_start(number, src, dst):
        own = pltpu.make_async_copy(src.at[leaf_at], dst.at[leaf_at], own_sem.at[number])
        own.start()

        def send(i, carry):
            peer = lax.rem(leaf_at + i, LEAVES)
            pltpu.make_async_remote_copy(
                src_ref=src.at[peer],
                dst_ref=dst.at[leaf_at],
                send_sem=leaf_send.at[number],
                recv_sem=leaf_recv.at[number],
                device_id={"leaf": peer},
                device_id_type=MESH,
            ).start()
            return carry

        lax.fori_loop(1, LEAVES, send, 0)
        return own

    def leaf_wait(number, own, src, dst):
        own.wait()
        others = pl.ds(0, LEAVES - 1)
        pltpu.make_async_copy(dst.at[others], dst.at[others], leaf_recv.at[number]).wait()
        pltpu.make_async_copy(src.at[others], src.at[others], leaf_send.at[number]).wait()

    root_row = jnp.concatenate(
        [root_ref[...].astype(F32), jnp.zeros((1, 32), F32)], axis=1
    )
    for half in range(2):
        turned[half * 128 : half * 128 + 128, :] = (
            up_ref[:, half * 128 : half * 128 + 128].astype(F32).T
        )
    for d in range(LEAVES):
        s1[d, 0:4, :] = turned[4 * d : 4 * d + 4, :]
        s1[d, 4:5, :] = root_row
    pl.semaphore_wait(barrier, LEAVES - 1 + SIDES - 1)
    own1 = leaf_start(0, s1, r1)
    br_copies = []
    for i in range(1, SIDES):
        peer = lax.rem(hand_at + i, SIDES)
        copy = pltpu.make_async_remote_copy(
            src_ref=br_ref,
            dst_ref=br_all.at[hand_at],
            send_sem=b_send.at[i],
            recv_sem=b_recv.at[i],
            device_id={"hand": peer},
            device_id_type=MESH,
        )
        copy.start()
        br_copies.append(copy)
    br_all[hand_at] = br_ref[...]

    low_r, high_r = cards_ref[0:1, :], cards_ref[1:2, :]

    def strip(i, carry):
        rows = pl.ds(pl.multiple_of(i * 16, 16), 16)
        low_c = jnp.broadcast_to(card_col_ref[rows, 0:1], (16, 1024))
        high_c = jnp.broadcast_to(card_col_ref[rows, 1:2], (16, 1024))
        share = card_hits(low_c, low_r, high_r) | card_hits(high_c, low_r, high_r)
        keep = jnp.where(share, 0.0, 1.0)
        apart[rows, :] = keep.astype(BF16)
        minus[rows, :] = (0.0 - keep).astype(BF16)
        return carry

    lax.fori_loop(0, 64, strip, 0)
    for g in range(3):
        rows = pl.ds(pl.multiple_of(hand_at * 24 + g * 8, 8), 8)
        for m in range(8):
            column[g, m * 128 : m * 128 + 128, 0:8] = (
                rank_ref[rows, m * 128 : m * 128 + 128].astype(F32).T
            )
        hit = jnp.zeros((8, 1024), F32)
        for c in range(5):
            card = jnp.broadcast_to(board_ref[rows, c : c + 1], (8, 1024))
            hit = jnp.where(card_hits(card, low_r, high_r), 1.0, hit)
        compat_all[g * 8 : g * 8 + 8, :] = (1.0 - hit) * PAYOFF_UNIT
    lane_row = lax.broadcasted_iota(I32, (128, 128), 0)
    for k in range(3):
        for t in range(16):
            index = parent_ref[k : k + 1, t * 128 : t * 128 + 128] & 127
            right_up[k, :, t * 128 : t * 128 + 128] = jnp.where(
                jnp.broadcast_to(index, (128, 128)) == lane_row, 1.0, 0.0
            ).astype(BF16)

    leaf_wait(0, own1, s1, r1)

    low_half = lax.broadcasted_iota(I32, (8, 128), 0) < 4
    place8 = lax.broadcasted_iota(I32, (8, 128), 1) // 32
    for m in range(8):
        pairs = [
            jnp.concatenate([r1[4 * m + q, 0:4, :], r1[32 + 4 * m + q, 0:4, :]], axis=0)
            for q in range(4)
        ]
        for level in range(4):
            out = jnp.zeros((8, 128), F32)
            for q in range(4):
                shift = ((q - level) * 32) % 128
                moved = pairs[q] if shift == 0 else pltpu.roll(pairs[q], shift, 1)
                out = jnp.where(place8 == q, moved, out)
            if level == 0:
                now_ref[:, m * 128 : m * 128 + 128] = out
            else:
                weights[level - 1, :, m * 128 : m * 128 + 128] = out

    def tables():
        first, second = [], []
        for m in range(8):
            here = now_ref[:, m * 128 : (m + 1) * 128]
            swapped = pltpu.roll(here, 4, 0)
            first.append(jnp.where(low_half, here, swapped))
            second.append(jnp.where(low_half, swapped, here))
        return first, second

    def wide_row(a, b):
        return jnp.where(low_half, jnp.broadcast_to(a, (8, 128)), jnp.broadcast_to(b, (8, 128)))

    for level in range(3):
        first, second = tables()
        for m in range(8):
            cut = slice(m * 128, (m + 1) * 128)
            index = wide_row(
                parent_ref[level : level + 1, m * 128 : m * 128 + 128],
                parent_ref[level : level + 1, 1024 + m * 128 : 1024 + m * 128 + 128],
            )
            now_ref[:, cut] = look_up(first, second, index) * weights[level, :, cut]
    first, second = tables()

    def reach_of(i, carry):
        index = wide_row(r1[2 * i, 4:5, :], r1[2 * i + 1, 4:5, :]).astype(I32)
        out = look_up(first, second, index)
        s2[2 * i] = out[0:4]
        s2[2 * i + 1] = out[4:8]
        return carry

    lax.fori_loop(0, 32, reach_of, 0)
    own2 = leaf_start(1, s2, r2)

    w_copy.wait()
    lane64 = lax.broadcasted_iota(I32, (8, 128), 1)
    own_block = (lane64 // 8 == lax.broadcasted_iota(I32, (8, 128), 0)) & (lane64 < 64)
    inner = lane64 & 7

    def spread_code(s):
        code = jnp.concatenate([code_ref[s], jnp.zeros((8, 120), F32)], axis=1)
        return jnp.where(own_block, lane_take(code, inner), 0.0)[:, 0:64]

    def totals(i, carry):
        for k in range(8):
            s = i * 8 + k
            legal = jnp.where(spread_code(s) == 0.0, 0.0, 1.0).astype(BF16)
            inverse[s] = 1.0 / dot(legal, w_ref[s])
        return carry

    lax.fori_loop(0, 12, totals, 0)

    def target(i, carry):
        index = r1[i, 4:5, :].astype(I32) & 127
        right[i] = jnp.where(
            jnp.broadcast_to(index, (128, 128)) == lane_row, 1.0, 0.0
        ).astype(BF16)
        return carry

    lax.fori_loop(0, LEAVES, target, 0)
    mine = pl.ds(pl.multiple_of(hand_at * 256, 256), 256)
    low_m, high_m = cards_ref[0:1, mine], cards_ref[1:2, mine]
    for g in range(12):
        hit = jnp.zeros((8, 256), F32)
        for c in range(5):
            card = jnp.broadcast_to(board_ref[g * 8 : g * 8 + 8, c : c + 1], (8, 256))
            hit = jnp.where(card_hits(card, low_m, high_m), 1.0, hit)
        board_sum[g * 8 : g * 8 + 8, :] = (1.0 - hit) * opp_ref[...]

    leaf_wait(1, own2, s2, r2)

    for d in range(LEAVES):
        turned[4 * d : 4 * d + 4, :] = r2[d]
    for half in range(2):
        cut = slice(half * 128, half * 128 + 128)
        reach_ref[:, cut] = turned[cut, :].T[0:96, :] * board_sum[0:96, cut]

    def leaf_group(dst, base, g):
        for k in range(8):
            s = base + g * 8 + k
            code = spread_code(s)
            stake = jnp.abs(code)
            high = jnp.floor(stake * 0.0625) * 16.0
            low = stake - high
            shown = code < 0.0
            coef = jnp.concatenate(
                [
                    jnp.where(shown, high, 0.0),
                    jnp.where(shown, low, 0.0),
                    jnp.where(shown, 0.0, high),
                    jnp.where(shown, 0.0, low),
                ],
                axis=0,
            ).astype(BF16)
            factor = reach_ref[pl.ds(s, 1), :] * inverse[s]
            wide = w_ref[s].astype(F32).reshape(8, 8, 256) * factor[:, None, :]
            y = dot(coef, wide.reshape(64, 256).astype(BF16))
            y1 = y[0:8] + y[8:16]
            y0 = y[16:24] + y[24:32]
            high1 = y1.astype(BF16).astype(F32)
            high0 = y0.astype(BF16).astype(F32)
            dst[g * 8 + k, 0:16, :] = jnp.concatenate([high1, y1 - high1], axis=0).astype(BF16)
            dst[g * 8 + k, 16:32, :] = jnp.concatenate([high0, y0 - high0], axis=0).astype(BF16)

    y_copies = []
    for i in (2, 1, 3):
        peer = lax.rem(hand_at + i, SIDES)

        def group_of(g, carry):
            leaf_group(sy.at[peer], peer * 24, g)
            return carry

        lax.fori_loop(0, 3, group_of, 0)
        copy = pltpu.make_async_remote_copy(
            src_ref=sy.at[peer],
            dst_ref=ry.at[hand_at],
            send_sem=y_send.at[i],
            recv_sem=y_recv.at[i],
            device_id={"hand": peer},
            device_id_type=MESH,
        )
        copy.start()
        y_copies.append(copy)

    def group_own(g, carry):
        leaf_group(ry.at[hand_at], hand_at * 24, g)
        return carry

    lax.fori_loop(0, 3, group_own, 0)

    def one_pass(q, first_pass):
        base = q * 256

        def group_of(g, carry):
            rows24 = pl.ds(pl.multiple_of(hand_at * 24 + g * 8, 8), 8)
            ranks = rank_ref[rows24, :].astype(F32)
            lows = ry[q, pl.ds(pl.multiple_of(g * 8, 8), 8), 16:32, :].reshape(128, 256)
            fold = dot(lows, apart[pl.ds(pl.multiple_of(base, 256), 256), :])
            for s in range(8):
                for part in range(16):
                    at = pl.multiple_of(base + part * 16, 16)
                    gap = ranks[s : s + 1] - column[g, pl.ds(at, 16), s : s + 1]
                    sign[s % 2, part * 16 : part * 16 + 16, :] = jnp.maximum(
                        jnp.minimum(gap.astype(BF16), apart[pl.ds(at, 16), :]),
                        minus[pl.ds(at, 16), :],
                    )
                total = dot(ry[q, g * 8 + s, 0:16, :], sign[s % 2])
                node = total[0:8] + total[8:16]
                node = node + (fold[s * 16 : s * 16 + 8] + fold[s * 16 + 8 : s * 16 + 16])
                if not first_pass:
                    node = node + node_ref[g * 8 + s]
                node_ref[g * 8 + s] = node
            return carry

        lax.fori_loop(0, 3, group_of, 0)

    one_pass(hand_at, True)
    for i, copy in zip((1, 3, 2), (y_copies[1], y_copies[2], y_copies[0])):
        copy.wait_recv()
        one_pass(lax.rem(hand_at + SIDES - i, SIDES), False)
    for copy in y_copies:
        copy.wait_send()
    for copy in br_copies:
        copy.wait()

    act_row = lax.broadcasted_iota(I32, (8, 1024), 0)

    def best_of(g, carry):
        for k in range(8):
            s = g * 8 + k
            value = node_ref[s] * compat_all[pl.ds(s, 1), :]
            value = jnp.where(act_row < br_act[hand_at * 24 + s], value, -1e30)
            sub_ref[pl.ds(s, 1), :] = jnp.max(value, axis=0, keepdims=True)
        return carry

    lax.fori_loop(0, 3, best_of, 0)
    board_total = jnp.sum(sub_ref[...], axis=0, keepdims=True)
    weighted = jnp.zeros((1, 256), F32)
    range_sum = jnp.zeros((1, 256), F32)
    for p in range(SIDES):
        weighted += board_total[:, p * 256 : p * 256 + 256] * br_all[p]
        range_sum += br_all[p]
    for p in range(SIDES):
        sx[p, 0:24, :] = sub_ref[:, p * 256 : p * 256 + 256]
        sx[p, 24:25, :] = weighted
    rx[hand_at] = sx[hand_at]
    x_copies = []
    for i in (2, 1, 3):
        peer = lax.rem(hand_at + i, SIDES)
        copy = pltpu.make_async_remote_copy(
            src_ref=sx.at[peer],
            dst_ref=rx.at[hand_at],
            send_sem=x_send.at[i],
            recv_sem=x_recv.at[i],
            device_id={"hand": peer},
            device_id_type=MESH,
        )
        copy.start()
        x_copies.append(copy)
    for copy in x_copies:
        copy.wait()

    for p in range(SIDES):
        board_sum[p * 24 : p * 24 + 24, :] = rx[p, 0:24, :]
    board_sum[96:128, :] = jnp.zeros((32, 256), F32)
    sides = (rx[0, 24:25, :] + rx[1, 24:25, :]) + (rx[2, 24:25, :] + rx[3, 24:25, :])
    side_row = sides[:, 0:128] + sides[:, 128:256]
    for half in range(2):
        cut = slice(half * 128, half * 128 + 128)
        turned[cut, :] = board_sum[:, cut].T
    for d in range(LEAVES):
        s3[d, 0:4, :] = turned[4 * d : 4 * d + 4, :]
        s3[d, 4:5, :] = side_row
    own3 = leaf_start(2, s3, r3)
    leaf_wait(2, own3, s3, r3)

    upper = lax.broadcasted_iota(I32, (8, 128), 0) // 4

    def choose(values, index, put):
        twice = jnp.concatenate([values, values], axis=0)
        high = twice.astype(BF16).astype(F32)
        low = twice - high
        big = jnp.broadcast_to(index >> 7, (8, 128))
        for i in range(4):
            is_a, is_b = big == 4 * i + upper, big == 4 * i + 2 + upper
            put(
                i * 16,
                jnp.concatenate(
                    [jnp.where(is_a, high, 0.0), jnp.where(is_b, high, 0.0)], axis=0
                ).astype(BF16),
            )
            put(
                64 + i * 16,
                jnp.concatenate(
                    [jnp.where(is_a, low, 0.0), jnp.where(is_b, low, 0.0)], axis=0
                ).astype(BF16),
            )

    def from_boards(j, carry):
        for k in range(4):
            i = j * 4 + k

            def put(row, block):
                left[i, row : row + 16, :] = block

            choose(r3[i, 0:4, :], r1[i, 4:5, :].astype(I32), put)
        return carry

    lax.fori_loop(0, 16, from_boards, 0)
    acc = jnp.zeros((128, 128), F32)
    for i in range(0, LEAVES, 2):
        acc = acc + dot_t(
            jnp.concatenate([left[i], left[i + 1]], axis=1),
            jnp.concatenate([right[i], right[i + 1]], axis=1),
        )
    levels = [None] * 4
    levels[3] = acc[0:64] + acc[64:128]
    for level in range(2, -1, -1):
        for t in range(16):

            def put(row, block, t=t):
                left[t, row : row + 16, :] = block

            choose(
                levels[level + 1][4 * t : 4 * t + 4],
                parent_ref[level : level + 1, t * 128 : t * 128 + 128],
                put,
            )
        acc = jnp.zeros((128, 128), F32)
        for t in range(0, 16, 2):
            acc = acc + dot_t(
                jnp.concatenate([left[t], left[t + 1]], axis=1),
                right_up[level, :, t * 128 : t * 128 + 256],
            )
        levels[level] = acc[0:64] + acc[64:128]

    column_sum = jnp.zeros((8, 128), F32)
    for t in range(8):
        column_sum = column_sum + levels[0][8 * t : 8 * t + 8]
    column_sum = column_sum[0:4] + column_sum[4:8]
    root4 = jnp.sum(column_sum, axis=1, keepdims=True) * (1.0 / 2048.0)
    spot = lax.rem(leaf_at, 32) * 4
    lane4 = lax.broadcasted_iota(I32, (4, 128), 1)
    at4 = lane4 == lax.broadcasted_iota(I32, (4, 128), 0) + spot
    placed = jnp.sum(jnp.where(at4, root4, 0.0), axis=0, keepdims=True)
    is_second = jnp.broadcast_to(leaf_at // 32, (1, 128)) == 1
    row_a = jnp.where(is_second, 0.0, placed)
    row_b = jnp.where(is_second, placed, 0.0)
    place64 = lax.broadcasted_iota(I32, (64, 128), 1) // 32
    for q in range(4):
        out = jnp.zeros((64, 128), F32)
        for level in range(4):
            shift = ((level - q) * 32) % 128
            moved = levels[level] if shift == 0 else pltpu.roll(levels[level], shift, 1)
            out = jnp.where(place64 == level, moved, out)
        for t in range(16):
            s4[4 * t + q, 0:4, :] = out[4 * t : 4 * t + 4]
            s4[4 * t + q, 4:5, :] = row_a
            s4[4 * t + q, 5:6, :] = row_b
    own4 = leaf_start(3, s4, r4)
    best_sum = jnp.zeros((1, 128), F32)
    for d in range(LEAVES):
        best_sum = best_sum + r3[d, 4:5, :]
    numerator = jnp.sum(best_sum, axis=1, keepdims=True) * (1.0 / 2048.0)
    denominator = jnp.sum(range_sum, axis=1, keepdims=True)
    best_ref[...] = numerator / denominator
    leaf_wait(3, own4, s4, r4)
    value_a = jnp.zeros((1, 128), F32)
    value_b = jnp.zeros((1, 128), F32)
    for d in range(LEAVES):
        turned[4 * d : 4 * d + 4, :] = r4[d, 0:4, :]
        value_a = value_a + r4[d, 4:5, :]
        value_b = value_b + r4[d, 5:6, :]
    value_ref[:, 0:128] = value_a
    value_ref[:, 128:256] = value_b
    for half in range(2):
        cut = slice(half * 128, half * 128 + 128)
        level_ref[:, cut] = turned[cut, :].T


def hand_cards(number):
    low_list = []
    high_list = []
    for low_card in range(52):
        for high_card in range(low_card + 1, 52):
            low_list.append(low_card)
            high_list.append(high_card)
    chosen = np.arange(number) * 1326 // number
    return np.stack([np.array(low_list)[chosen], np.array(high_list)[chosen]]).astype(np.int32)


def local(
    opp_range,
    br_range,
    up_weight,
    up_parent,
    board_cards,
    hand_rank,
    root_parent,
    br_actions,
    opp_actions,
    leaf_kind,
    leaf_stake,
    opp_weight,
):
    cards = hand_cards(1024)
    legal = jnp.arange(8)[None, None, :] < opp_actions[:, :, None]
    code = jnp.where(legal, jnp.where(leaf_kind == 1, -leaf_stake, leaf_stake), 0).astype(F32)
    vmem = pl.BlockSpec(memory_space=VMEM)
    level_out, root_value, best = pl.pallas_call(
        kernel,
        out_shape=(
            jax.ShapeDtypeStruct((128, 256), F32),
            jax.ShapeDtypeStruct((1, 256), F32),
            jax.ShapeDtypeStruct((1, 1), F32),
        ),
        in_specs=[pl.BlockSpec(memory_space=pltpu.SMEM)]
        + [vmem] * 10
        + [pl.BlockSpec(memory_space=pl.ANY)],
        out_specs=(vmem, vmem, vmem),
        scratch_shapes=[
            VMEM((96, 64, 256), BF16),
            VMEM((1024, 1024), BF16),
            VMEM((1024, 1024), BF16),
            VMEM((2, 256, 1024), BF16),
            VMEM((LEAVES, 5, 128), F32),
            VMEM((LEAVES, 5, 128), F32),
            VMEM((LEAVES, 4, 128), F32),
            VMEM((LEAVES, 4, 128), F32),
            VMEM((LEAVES, 5, 128), F32),
            VMEM((LEAVES, 5, 128), F32),
            VMEM((LEAVES, 6, 128), F32),
            VMEM((LEAVES, 6, 128), F32),
            VMEM((SIDES, 24, 32, 256), BF16),
            VMEM((SIDES, 24, 32, 256), BF16),
            VMEM((SIDES, 25, 256), F32),
            VMEM((SIDES, 25, 256), F32),
            VMEM((SIDES, 1, 256), F32),
            VMEM((3, 8, 1024), F32),
            VMEM((8, 1024), F32),
            VMEM((256, 128), F32),
            VMEM((128, 256), F32),
            VMEM((96, 256), F32),
            VMEM((96, 8, 256), F32),
            VMEM((3, 1024, 8), F32),
            VMEM((24, 8, 1024), F32),
            VMEM((24, 1024), F32),
            VMEM((24, 1024), F32),
            VMEM((LEAVES, 128, 128), BF16),
            VMEM((LEAVES, 128, 128), BF16),
            VMEM((3, 128, 2048), BF16),
            pltpu.SemaphoreType.DMA((4,)),
            pltpu.SemaphoreType.DMA((4,)),
            pltpu.SemaphoreType.DMA((4,)),
            pltpu.SemaphoreType.DMA,
            pltpu.SemaphoreType.DMA((4,)),
            pltpu.SemaphoreType.DMA((4,)),
            pltpu.SemaphoreType.DMA((4,)),
            pltpu.SemaphoreType.DMA((4,)),
            pltpu.SemaphoreType.DMA((4,)),
            pltpu.SemaphoreType.DMA((4,)),
        ],
        compiler_params=pltpu.CompilerParams(collective_id=0, has_side_effects=True),
        name="tree",
    )(
        br_actions,
        up_weight.reshape(128, 256),
        root_parent.reshape(1, 96),
        up_parent,
        opp_range.reshape(1, 256),
        br_range.reshape(1, 256),
        jnp.asarray(cards),
        jnp.asarray(cards.T),
        board_cards,
        hand_rank,
        code,
        opp_weight.reshape(96, 64, 256),
    )
    return level_out.reshape(4, 32, 256), root_value.reshape(256), best[0, 0]


def solution(mesh):
    in_specs = (
        P("hand"),
        P("hand"),
        P(None, "leaf", "hand"),
        P(),
        P("leaf", None),
        P("leaf", None),
        P("leaf"),
        P("leaf"),
        P("leaf", None),
        P("leaf", None, None),
        P("leaf", None, None),
        P("leaf", None, None, "hand"),
    )
    out_specs = (P(None, "leaf", "hand"), P("hand"), P())
    return jax.shard_map(local, mesh=mesh, in_specs=in_specs, out_specs=out_specs, check_vma=False)
```

time: 496 us -> 103 us (0.21)
  waiting for transfers between devices: 238 us -> 0 us
  Pallas kernels: 0 us -> 92.4 us
  blocking collectives: 83.1 us -> 0 us
  other arithmetic: 65.8 us -> 1.67 us
  matrix products: 37 us -> 0 us
  local copies, waits for them, and re-layouts: 40.1 us -> 6.12 us
  between operations: 16.5 us -> 2.42 us
  starting transfers between devices: 14 us -> 0 us
    all_gather x3 -> x0, waiting for transfers between devices: 180 us -> none  [the longest x1 122 us: local(): block_rows = lax.all_gather(leaf_reach, 'hand', axis=2, tiled=True)]
    pallas_call x0 -> x1, Pallas kernels: none -> 92.4 us  [local(): pl.pallas_call(kernel, out_shape=(jax.ShapeDtypeStruct((128, 256), F32),...]
    all_to_all x1 -> x0, blocking collectives: 62.1 us -> none  [summed_on_arrival(): lax.all_to_all(parts, axis, split_axis=0, concat_axis=0, tiled=True)]
    all_to_all x2 -> x0, waiting for transfers between devices: 58.3 us -> none  [copy_for_each(): lax.all_to_all(jnp.broadcast_to(x[None], (devices, *x.shape)), axis, 0, 0...]
    scatter-add x4 -> x0, other arithmetic: 40.5 us -> none  [the longest x3 38.8 us: local(): jax.ops.segment_sum(whole_level, up_parent[level_id - 1], num_segments=no...]
    dot_general x2 -> x0, matrix products: 37 us -> none  [the longest x1 28.5 us: local(): jnp.einsum('blo,boh->blh', block_rows, order_sign, preferred_element_type...]
    gather x4 -> x0, local copies, waits for them, and re-layouts: 28.7 us -> none  [the longest x3 27.9 us: local(): jnp.take(gathered, up_parent[level_id - 1], axis=0)]
    all_to_all x2 -> x0, starting transfers between devices: 13.9 us -> none  [copy_for_each(): lax.all_to_all(jnp.broadcast_to(x[None], (devices, *x.shape)), axis, 0, 0...]
  transfers between devices with their start and end apart: 5 -> 0, of which waited for: 5 -> 0; matrix products, arithmetic and copies ran while one was open for 2% -> 0% of each run, Pallas kernels for 0% -> 0%
where the time goes in v2:
time: 103 us
  Pallas kernels  92.4 us (90%)
  local copies, waits for them, and re-layouts  6.12 us (6%)
  between operations  2.42 us (2%)
  other arithmetic  1.67 us (2%)
    pallas_call x1, Pallas kernels, local(): pl.pallas_call(kernel, out_shape=(jax.ShapeDtypeStruct((128, 256), F32),...  92.4 us
    unnamed x5, local copies, waits for them, and re-layouts  5.9 us

profile of v2, /device:TPU:1, one launch (start us, length us, event | category | flops | bytes accessed | tf_op | source)
XLA Modules:
  0.0 102.6 jit_solution(7278117563473807538)
XLA Ops:
  0.6 1.0 copy.24
  1.6 0.8 broadcast_compare_fusion
  2.4 0.2 copy.25
  2.6 0.8 copy.23
  3.4 0.9 fusion.1.code_ref
  4.3 1.4 %copy.27.board_ref = s32[96,5]{1,0:T(8,128)} copy(s32[96,5]{0,1:T(8,128)} %param.18) | data formatting | bytes 3840 | tf_op args[4]
  5.7 92.4 %tree.1 = (f32[128,256]{1,0:T(8,128)}, f32[1,256]{1,0:T(1,128)}, f32[1,1]{1,0:T(1,128)}) custom-call(s32[96]{0:T(128)} %br_act.1, bf16[128,256]{1,0:T(8,128)(2,1)} %bitcast.10, s32[1,96]{1,0:T(1,128)} %bitcast.14, s32[3,2048]{1,0:T(4,128)} %parent_ref.1, f32[1,256]{1,0:T(1,128)} %bitcast.11, f32[1,256]{1,0:T(1,128)} %bitcast.12, ...), custom_call_target="tpu_custom_call" | custom-call | tf_op jit(solution)/shard_map/tree/pallas_call | solution.py:574
  98.1 1.6 %copy.31 = f32[4,32,256]{2,1,0:T(8,128)} copy(f32[4,32,256]{2,1,0:T(8,128)} %bitcast.9) | data formatting | bytes 262144
  99.6 1.2 %copy.32 = f32[256]{0:T(256)} copy(f32[256]{0:T(256)} %bitcast.13) | data formatting | bytes 2048
